TPU v7x, 32 devices: a whole 2x2x4 slice. The times are simulated.
32 devices in a mesh: dp: 8 (over y, x, core), mp: 4 (over z).
Axes of the slice: x: 2, y: 2, z: 4, core: 2. Of those that a mesh axis runs over, the one named last changes fastest.
Arguments:
- states: bfloat16 [128, 80, 768], P('dp'), may hold values from -6 to 6
- hist_len: int32 [128], P('dp'), may hold values from 1 to 20
- norm_gain: float32 [768], replicated, may hold values from 0.5 to 1.5
- qkv_weight: bfloat16 [768, 3, 12, 64], P(None, None, 'mp'), may hold values from -1 to 1
- output_weight: bfloat16 [12, 64, 768], P('mp'), may hold values from -0.21875 to 0.21875
- cotangent: bfloat16 [128, 80, 768], P('dp'), may hold values from -6 to 6
Outputs:
- attended: bfloat16 [128, 80, 768], P('dp')
- grad_states: bfloat16 [128, 80, 768], P('dp')
- grad_qkv: float32 [768, 3, 12, 64], P('dp', None, 'mp')
- output_weight_gradient: float32 [12, 64, 768], P('mp', None, 'dp')
- grad_gain: float32 [768], P('dp')
All inputs are finite; a program needn't handle non-finite values.
Results may differ from a plain program's by a relative error of at most 0.012.
Values may be sent and summed in bfloat16 or wider, within the bound.
A program may use at most 128 MiB of HBM per device.

v0:
```python
import jax
import jax.numpy as jnp
from jax import lax
from jax.sharding import PartitionSpec as P

LEVELS = 4


def body(states, hist_len, norm_gain, qkv_weight, output_weight, cotangent):
    wide_states = states.astype(jnp.float32)
    inv_rms = lax.rsqrt(jnp.mean(wide_states * wide_states, axis=-1, keepdims=True) + 1e-06)
    unit = wide_states * inv_rms
    normed = (unit * norm_gain).astype(jnp.bfloat16)
    proj = jnp.einsum(
        "bsd,dchk->bschk", normed, qkv_weight, preferred_element_type=jnp.float32
    ).astype(jnp.bfloat16)
    queries = proj[:, :, 0]
    key_rows = proj[:, :, 1]
    value_rows = proj[:, :, 2]
    positions = jnp.arange(states.shape[1], dtype=jnp.int32)
    keep_mask = positions[None, :] < LEVELS * hist_len[:, None]
    scores = jnp.einsum("bqhk,bphk->bhqp", queries, key_rows, preferred_element_type=jnp.float32)
    masked = jnp.where(keep_mask[:, None, None, :], scores, -1e30)
    row_top = jnp.max(masked, axis=-1, keepdims=True)
    exp_scores = jnp.exp(masked - row_top)
    attn_prob = exp_scores / jnp.sum(exp_scores, axis=-1, keepdims=True)
    prob_bf = attn_prob.astype(jnp.bfloat16)
    attended_context = jnp.einsum(
        "bhqp,bphk->bqhk", prob_bf, value_rows, preferred_element_type=jnp.float32
    ).astype(jnp.bfloat16)
    partial_mix = jnp.einsum(
        "zagm,gms->zas", attended_context, output_weight, preferred_element_type=jnp.float32
    )
    mixed_total_sum = lax.psum(partial_mix.astype(jnp.bfloat16), "mp").astype(jnp.float32)
    attended = (wide_states + mixed_total_sum).astype(jnp.bfloat16)
    masked_cotangent = jnp.where(keep_mask[:, :, None], cotangent, jnp.zeros_like(cotangent))
    local_output = jnp.einsum(
        "wmep,wmx->epx", attended_context, masked_cotangent, preferred_element_type=jnp.float32
    )
    context_gradient = jnp.einsum(
        "uxy,wgy->uxwg", masked_cotangent, output_weight, preferred_element_type=jnp.float32
    ).astype(jnp.bfloat16)
    grad_prob = jnp.einsum(
        "bqhk,bphk->bhqp", context_gradient, value_rows, preferred_element_type=jnp.float32
    )
    row_delta = jnp.sum(attn_prob * grad_prob, axis=-1, keepdims=True)
    grad_score = (attn_prob * (grad_prob - row_delta)).astype(jnp.bfloat16)
    grad_query = jnp.einsum(
        "bhqp,bphk->bqhk", grad_score, key_rows, preferred_element_type=jnp.float32
    )
    grad_key = jnp.einsum(
        "bhqp,bqhk->bphk", grad_score, queries, preferred_element_type=jnp.float32
    )
    grad_value = jnp.einsum(
        "bhqp,bqhk->bphk", prob_bf, context_gradient, preferred_element_type=jnp.float32
    )
    grad_proj = jnp.stack([grad_query, grad_key, grad_value], axis=2).astype(jnp.bfloat16)
    local_qkv = jnp.einsum("bsd,bschk->dchk", normed, grad_proj, preferred_element_type=jnp.float32)
    partial_normed = jnp.einsum(
        "bschk,dchk->bsd", grad_proj, qkv_weight, preferred_element_type=jnp.float32
    )
    wide_cot = masked_cotangent.astype(jnp.float32)
    grad_normed = lax.psum(partial_normed, "mp")
    local_gain = jnp.sum(grad_normed * unit, axis=(0, 1))
    unit_grad = grad_normed * norm_gain
    row_corr = jnp.mean(unit_grad * unit, axis=-1, keepdims=True)
    grad_states = (wide_cot + inv_rms * (unit_grad - unit * row_corr)).astype(jnp.bfloat16)
    grad_qkv, output_weight_gradient, grad_gain = (
        lax.psum_scatter(local_qkv, "dp", scatter_dimension=0, tiled=True),
        lax.psum_scatter(local_output, "dp", scatter_dimension=2, tiled=True),
        lax.psum_scatter(local_gain, "dp", scatter_dimension=0, tiled=True),
    )
    return (attended, grad_states, grad_qkv, output_weight_gradient, grad_gain)


def solution(mesh):
    placed = (
        P("dp", None, None),
        P("dp"),
        P(),
        P(None, None, "mp", None),
        P("mp", None, None),
        P("dp", None, None),
    )
    return jax.shard_map(
        body,
        mesh=mesh,
        in_specs=placed,
        out_specs=(
            P("dp", None, None),
            P("dp", None, None),
            P("dp", None, "mp", None),
            P("mp", None, "dp"),
            P("dp"),
        ),
        check_vma=False,
    )
```

profile of v0, /device:TPU:0, one launch (start us, length us, event | category | flops | bytes accessed | tf_op | source)
XLA Modules:
  0.0 289.7 jit_solution(6222700549356190898)
XLA Ops:
  8.0 0.0 copy-start
  8.0 0.0 copy-start.1
  8.0 0.0 copy-start.9
  8.0 0.0 reduce-scatter.9.cloned.1.call-start
  8.1 0.8 broadcast_multiply_fusion.1
  8.9 0.1 iota_compare_fusion
  9.0 2.0 fusion.12
  11.0 0.0 copy-done
  11.0 3.4 %convolution_convert_fusion = bf16[16,80,3,3,64]{1,4,3,2,0:T(8,128)(2,1)} fusion(bf16[16,80,768]{2,1,0:T(8,128)(2,1)S(1)} %copy-done.1, f32[768]{0:T(1024)S(1)} %copy-done.9, f32[16,80]{1,0:T(8,128)S(1)} %add_rsqrt_fusion, bf16[768,3,3,64]{0,3,2,1:T(8,128)(2,1)S(1)} %copy-done), kind=kOutput, calls=%fused_computation.20 | convolution fusion | flops 1137131520 | bytes 4333568 | tf_op jit(solution)/shard_map/bsd,dchk->bschk/dot_general | solution.py:14
  14.5 3.6 %fusion.51 = (f32[16,3,80]{2,1,0:T(4,128)S(1)}, f32[16,3,80,80]{2,3,1,0:T(8,128)}) fusion(pred[16,80]{1,0:T(8,128)(4,1)S(1)} %iota_compare_fusion, bf16[16,80,3,3,64]{1,4,3,2,0:T(8,128)(2,1)} %convolution_convert_fusion), kind=kOutput, calls=%fused_computation.69 | convolution fusion | flops 40243280 | bytes 2818304 | tf_op jit(solution)/shard_map/sub | solution.py:25
  18.1 2.3 fusion.27
  20.4 0.9 copy-done.5
  21.4 0.9 fusion.31
  22.3 1.5 copy.40
  23.8 2.7 reshape.73
  26.5 0.0 reduce-scatter.9.cloned.1.call-update
  26.5 0.0 reduce-scatter.7.cloned.1.call-start
  26.6 0.0 copy-start.3
  26.6 2.6 fusion.24
  29.2 0.6 fusion.30
  29.9 1.0 copy-done.4
  30.9 0.6 multiply_reduce_fusion
  31.5 0.5 multiply_convert_fusion
  32.0 0.4 fusion.28
  32.4 0.6 fusion.29
  33.0 0.0 copy-done.11
  33.0 3.0 %fusion.14 = f32[768,3,3,64,1]{0,3,2,4,1:T(8,128)} fusion(bf16[16,80,768]{2,1,0:T(8,128)(2,1)S(1)} %copy-done.1, f32[768]{0:T(1024)S(1)} %copy-done.9, f32[16,80]{1,0:T(8,128)S(1)} %add_rsqrt_fusion, bf16[16,80,1,3,64]{1,4,3,0,2:T(8,128)(2,1)S(1)} %fusion.30, bf16[16,80,1,3,64]{1,4,3,0,2:T(8,128)(2,1)S(1)} %fusion.29, ...), kind=kOutput, calls=%fused_computation.21 | convolution fusion | flops 1140817920 | bytes 5218304 | tf_op jit(solution)/shard_map/bsd,bschk->dchk/dot_general | solution.py:58
  36.0 2.8 copy.42
  38.8 0.0 reduce-scatter.7.cloned.1.call-update
  38.9 0.0 all-reduce.6.cloned.1.call-start
  38.9 5.4 %convolution_bitcast_fusion = f32[16,80,768]{2,1,0:T(8,128)} fusion(bf16[16,80,1,3,64]{1,4,3,0,2:T(8,128)(2,1)} %copy-done.11, bf16[16,80,1,3,64]{1,4,3,0,2:T(8,128)(2,1)} %copy-done.7, bf16[16,80,1,3,64]{1,4,3,0,2:T(8,128)(2,1)} %copy-done.6, bf16[768,3,3,64]{0,3,2,1:T(8,128)(2,1)S(1)} %copy-done), kind=kOutput, calls=%fused_computation.19 | convolution fusion | flops 1133936640 | bytes 6291456 | tf_op jit(solution)/shard_map/bschk,dchk->bsd/dot_general | solution.py:59
  44.3 0.0 all-reduce.6.cloned.1.call-update
  44.3 0.0 copy-start.10
  44.3 0.2 all-reduce.4.cloned.1.call-start
  44.6 3.2 %bitcast_convert_fusion = bf16[16,80,768]{2,1,0:T(8,128)(2,1)} fusion(bf16[16,80,3,64]{1,3,2,0:T(8,128)(2,1)} %copy-done.5, bf16[3,64,768]{2,1,0:T(8,128)(2,1)S(1)} %copy-done.8), kind=kOutput, calls=%fused_computation.17 | convolution fusion | flops 378470400 | bytes 2752512 | tf_op jit(solution)/shard_map/zagm,gms->zas/dot_general | solution.py:31
  47.8 0.0 all-reduce.4.cloned.1.call-update
  47.8 0.6 dynamic-slice
  49.1 15.3 %reduce-scatter.9.cloned.1.call-done = f32[96,192]{1,0:T(8,128)} async-done(((f32[768,192]{1,0:T(8,128)}), f32[96,192]{1,0:T(8,128)}) %reduce-scatter.9.cloned.1.call-update) | async-done | bytes 73744
  64.3 1.0 reshape.74
  65.4 0.8 copy.41
  66.1 42.4 %reduce-scatter.7.cloned.1.call-done = f32[96,576]{1,0:T(8,128)} async-done(((f32[768,576]{1,0:T(8,128)}), f32[96,576]{1,0:T(8,128)}) %reduce-scatter.7.cloned.1.call-update) | async-done | bytes 221200
  108.5 1.8 copy.43
  110.3 83.2 %all-reduce.6.cloned.1.call-done = f32[16,80,768]{2,1,0:T(8,128)} async-done(((f32[16,80,768]{2,1,0:T(8,128)}), f32[16,80,768]{2,1,0:T(8,128)}) %all-reduce.6.cloned.1.call-update) | async-done | bytes 3932176 | tf_op jit(solution)/shard_map/psum | solution.py:63
  193.4 3.2 %fusion.11 = (f32[768]{0:T(1024)S(1)}, f32[16,80]{1,0:T(8,128)S(1)}) fusion(f32[16,80,768]{2,1,0:T(8,128)} %all-reduce.6.cloned.1.call-done, bf16[16,80,768]{2,1,0:T(8,128)(2,1)S(1)} %copy-done.1, f32[16,80]{1,0:T(8,128)S(1)} %add_rsqrt_fusion, f32[768]{0:T(1024)S(1)} %copy-done.9), kind=kLoop, calls=%fused_computation.14 | loop fusion | flops 6879232 | bytes 5914624 | tf_op jit(solution)/shard_map/reduce_sum | solution.py:64
  196.7 13.8 %all-reduce = f32[768]{0:T(1024)S(1)} all-reduce(f32[768]{0:T(1024)S(1)} %get-tuple-element.5), channel_id=4, replica_groups=mesh['dp'=8,'mp'=4] {'dp'}, use_global_device_ids=true, to_apply=%region_10.11.clone | all-reduce | flops 768 | bytes 6144
  210.5 0.6 dynamic-slice.1
  211.1 65.9 %all-reduce.4.cloned.1.call-done = bf16[16,80,768]{2,1,0:T(8,128)(2,1)} async-done(((bf16[16,80,768]{2,1,0:T(8,128)(2,1)}), bf16[16,80,768]{2,1,0:T(8,128)(2,1)}) %all-reduce.4.cloned.1.call-update) | async-done | bytes 1966096 | tf_op jit(solution)/shard_map/psum | solution.py:34
  277.0 5.3 %fusion.10 = (bf16[16,80,768]{2,1,0:T(8,128)(2,1)}, bf16[16,80,768]{2,1,0:T(8,128)(2,1)}) fusion(bf16[16,80,768]{2,1,0:T(8,128)(2,1)S(1)} %copy-done.1, f32[16,80,768]{2,1,0:T(8,128)} %all-reduce.6.cloned.1.call-done, f32[16,80]{1,0:T(8,128)S(1)} %broadcast_multiply_fusion, f32[768]{0:T(1024)S(1)} %copy-done.9, f32[16,80]{1,0:T(8,128)S(1)} %add_rsqrt_fusion, ...), kind=kLoop, calls=%fused_computation.13 | loop fusion | flops 12779520 | bytes 13777152 | tf_op jit(solution)/shard_map/convert_element_type | solution.py:67
  (17 shorter events, 0.0 us)
Async XLA Ops:
  8.0 3.0 %copy-start = (bf16[768,3,3,64]{0,3,2,1:T(8,128)(2,1)S(1)}, bf16[768,3,3,64]{0,3,2,1:T(8,128)(2,1)}, u32[]{:S(2)}) copy-start(bf16[768,3,3,64]{0,3,2,1:T(8,128)(2,1)} %param.9) | copy-start | bytes 2654212
  8.0 3.0 %copy-start.1 = (bf16[16,80,768]{2,1,0:T(8,128)(2,1)S(1)}, bf16[16,80,768]{2,1,0:T(8,128)(2,1)}, u32[]{:S(2)}) copy-start(bf16[16,80,768]{2,1,0:T(8,128)(2,1)} %param.6) | copy-start | bytes 5898244
  8.0 3.0 %copy-start.9 = (f32[768]{0:T(1024)S(1)}, f32[768]{0:T(1024)}, u32[]{:S(2)}) copy-start(f32[768]{0:T(1024)} %param.8) | copy-start | bytes 9220
  8.0 56.3 %reduce-scatter.9.cloned.1.call-start = ((), (), s32[]{:S(2)}) async-start(), calls=%async_computation.5 | async-start | bytes 884736
  18.1 3.3 %copy-start.2 = (bf16[16,80,768]{2,1,0:T(8,128)(2,1)S(1)}, bf16[16,80,768]{2,1,0:T(8,128)(2,1)}, u32[]{:S(2)}) copy-start(bf16[16,80,768]{2,1,0:T(8,128)(2,1)} %param.11) | copy-start | bytes 5898244
  20.4 0.9 copy-start.5
  23.8 2.8 copy-start.8
  26.5 82.0 %reduce-scatter.7.cloned.1.call-start = ((), (), s32[]{:S(2)}) async-start(), calls=%async_computation.4 | async-start | bytes 2211840
  26.6 2.6 copy-start.3
  29.2 1.7 copy-start.4
  30.9 2.1 copy-start.11
  32.4 3.6 %copy-start.6 = (bf16[16,80,1,3,64]{1,4,3,0,2:T(8,128)(2,1)}, bf16[16,80,1,3,64]{1,4,3,0,2:T(8,128)(2,1)S(1)}, u32[]{:S(2)}) copy-start(bf16[16,80,1,3,64]{1,4,3,0,2:T(8,128)(2,1)S(1)} %fusion.28) | copy-start | bytes 1474564
  33.0 3.0 %copy-start.7 = (bf16[16,80,1,3,64]{1,4,3,0,2:T(8,128)(2,1)}, bf16[16,80,1,3,64]{1,4,3,0,2:T(8,128)(2,1)S(1)}, u32[]{:S(2)}) copy-start(bf16[16,80,1,3,64]{1,4,3,0,2:T(8,128)(2,1)S(1)} %fusion.29) | copy-start | bytes 1474564
  38.9 154.6 %all-reduce.6.cloned.1.call-start = ((), (), s32[]{:S(2)}) async-start(), calls=%async_computation.3 | async-start | bytes 7864320 | tf_op jit(solution)/shard_map/psum | solution.py:63
  44.3 3.5 %copy-start.10 = (u32[32]{0:T(128)S(1)}, u32[32]{0:T(128)}, u32[]{:S(2)}) copy-start(u32[32]{0:T(128)} %constant.20) | copy-start | bytes 388
  44.3 232.6 %all-reduce.4.cloned.1.call-start = ((), (), s32[]{:S(2)}) async-start(), calls=%async_computation.2 | async-start | bytes 3932160 | tf_op jit(solution)/shard_map/psum | solution.py:34
Sparse Core Ops, SparseCore 0:
  26.6 37.6 reduce-scatter.8
  68.3 40.1 reduce-scatter.6
Sparse Core Ops, SparseCore 1:
  44.4 149.0 all-reduce.5
  196.3 80.6 all-reduce.3
where the time goes:
time: 290 us
  waiting for transfers between devices  207 us (71%)
  matrix products  26.7 us (9%)
  between operations  16.3 us (6%)
  local copies, waits for them, and re-layouts  13.8 us (5%)
  blocking collectives  13.8 us (5%)
  other arithmetic  12 us (4%)
    psum x1, waiting for transfers between devices, body(): grad_normed = lax.psum(partial_normed, 'mp')  83.2 us
    psum x1, waiting for transfers between devices, body(): lax.psum(partial_mix.astype(jnp.bfloat16), 'mp').astype(jnp.float32)  65.9 us
    unnamed x6, waiting for transfers between devices  57.7 us
    unnamed x1, blocking collectives  13.8 us
    unnamed x32, local copies, waits for them, and re-layouts  13.8 us
  transfers between devices with their start and end apart: 4, of which 4 were waited for; matrix products, arithmetic and copies ran while one was open for 10% of the time, Pallas kernels for 0%

commit v1 on v0

v1 whole, which is shorter than its diff:
```python
import functools

import jax
import jax.numpy as jnp
from jax import lax
from jax.experimental import pallas as pl
from jax.experimental.pallas import tpu as pltpu
from jax.sharding import PartitionSpec as P

LEVELS = 4
PIECES = 8
GROUP = 4
BF = jnp.bfloat16
F32 = jnp.float32
MESH = pl.DeviceIdType.MESH


def dot(a, b, ca, cb):
    return lax.dot_general(a, b, (((ca,), (cb,)), ((), ())), preferred_element_type=F32)


def remote(src, dst, ssem, rsem, device):
    return pltpu.make_async_remote_copy(
        src_ref=src, dst_ref=dst, send_sem=ssem, recv_sem=rsem, device_id=device, device_id_type=MESH
    )


def gather_kernel(n, own, wall, s_z, r_z, s_xy, r_xy, s_c, r_c):
    d, z = lax.axis_index("dp"), lax.axis_index("mp")
    c, bx, by = d % 2, (d // 2) % 2, (d // 4) % 2
    par = (bx + by) % 2
    partner = (d + 1 - 2 * c, z)
    across = ((d + 2 - 4 * bx, z), (d + 4 - 8 * by, z))
    barrier = pltpu.get_barrier_semaphore()
    greet = [(d, (z + n - j) % n) for j in range(1, n)] + list(across) + [partner]
    for device in greet:
        pl.semaphore_signal(barrier, inc=1, device_id=device, device_id_type=MESH)
    pl.semaphore_wait(barrier, len(greet))

    mine = [4 * par + 2 * i + c for i in range(2)]
    theirs = [4 * (1 - par) + 2 * i + c for i in range(2)]
    far = [4 * par + 2 * i + 1 - c for i in range(2)] + [4 * (1 - par) + 2 * i + 1 - c for i in range(2)]
    order = [j for j in (1, n - 1) if j < n] + [j for j in range(2, n - 1)]
    sends = []

    def go(src, dst, ssem, rsem, device):
        copy = remote(src, dst, ssem, rsem, device)
        copy.start()
        sends.append(copy)

    for j in order:
        for i in range(2):
            go(own.at[mine[i]], wall.at[j - 1, mine[i]], s_z.at[i, j - 1], r_z.at[i, j - 1], (d, (z + n - j) % n))
    for j in order:
        for i in range(2):
            spot = wall.at[j - 1, mine[i]]
            remote(spot, spot, s_z.at[i, j - 1], r_z.at[i, j - 1], partner).wait_recv()
            go(spot, spot, s_xy.at[i, j - 1], r_xy.at[i, j - 1], across[i])
            go(spot, spot, s_c.at[i, j - 1], r_c.at[i, j - 1], partner)
    for j in order:
        for i in range(2):
            spot = wall.at[j - 1, theirs[i]]
            remote(spot, spot, s_xy.at[i, j - 1], r_xy.at[i, j - 1], partner).wait_recv()
            go(spot, spot, s_c.at[2 + i, j - 1], r_c.at[2 + i, j - 1], partner)
    for j in order:
        for i in range(4):
            spot = wall.at[j - 1, far[i]]
            remote(spot, spot, s_c.at[i, j - 1], r_c.at[i, j - 1], partner).wait_recv()
    for copy in sends:
        copy.wait_send()


def gather(own, n):
    pairs = pltpu.SemaphoreType.DMA((2, n - 1))
    quads = pltpu.SemaphoreType.DMA((4, n - 1))
    return pl.pallas_call(
        functools.partial(gather_kernel, n),
        out_shape=jax.ShapeDtypeStruct((n - 1,) + own.shape, own.dtype),
        in_specs=[pl.BlockSpec(memory_space=pl.ANY)],
        out_specs=pl.BlockSpec(memory_space=pl.ANY),
        scratch_shapes=[pairs, pairs, pairs, pairs, quads, quads],
        compiler_params=pltpu.CompilerParams(collective_id=1, has_side_effects=True),
        name="gather",
    )(own)


def scatter_kernel(half, part, out, got, total, held, s_c, r_c, s_o, r_o):
    d, z = lax.axis_index("dp"), lax.axis_index("mp")
    c, chip = d % 2, d // 2
    partner = (d + 1 - 2 * c, z)
    others = [(((chip + o) % half) * 2 + c, z) for o in range(1, half)]
    barrier = pltpu.get_barrier_semaphore()
    for device in others + [partner]:
        pl.semaphore_signal(barrier, inc=1, device_id=device, device_id_type=MESH)
    pl.semaphore_wait(barrier, half)
    order = list(range(1, half)) + [0]
    sends = []
    for o in order:
        t = (chip + o) % half
        copy = remote(part.at[1 - c, t], got.at[o], s_c.at[o], r_c.at[o], partner)
        copy.start()
        sends.append(copy)
    for o in order:
        t = (chip + o) % half
        remote(got.at[o], got.at[o], s_c.at[o], r_c.at[o], partner).wait_recv()
        both = part[c, t].astype(F32) + got[o].astype(F32)
        if o == 0:
            out[...] = both
        else:
            total[o - 1] = both.astype(BF)
            copy = remote(total.at[o - 1], held.at[o - 1], s_o.at[o - 1], r_o.at[o - 1], others[o - 1])
            copy.start()
            sends.append(copy)
    for o in range(1, half):
        remote(held.at[o - 1], held.at[o - 1], s_o.at[o - 1], r_o.at[o - 1], partner).wait_recv()
        out[...] += held[o - 1].astype(F32)
    for copy in sends:
        copy.wait_send()


def scatter(part):
    _, half, rows, wide = part.shape
    return pl.pallas_call(
        functools.partial(scatter_kernel, half),
        out_shape=jax.ShapeDtypeStruct((rows, wide), F32),
        in_specs=[pl.BlockSpec(memory_space=pltpu.VMEM)],
        out_specs=pl.BlockSpec(memory_space=pltpu.VMEM),
        scratch_shapes=[
            pltpu.VMEM((half, rows, wide), BF),
            pltpu.VMEM((half - 1, rows, wide), BF),
            pltpu.VMEM((half - 1, rows, wide), BF),
            pltpu.SemaphoreType.DMA((half,)),
            pltpu.SemaphoreType.DMA((half,)),
            pltpu.SemaphoreType.DMA((half - 1,)),
            pltpu.SemaphoreType.DMA((half - 1,)),
        ],
        compiler_params=pltpu.CompilerParams(collective_id=2, has_side_effects=True),
        name="scatter",
    )(part)


def work_kernel(nb, n, width, hist, states, cot, gain, own, wall, att, gst, part,
                wq, wo, acc, gacc, proj, gproj, ctx, gctx, sems):
    i = pl.program_id(0)
    _, s, dim = states.shape
    rows = nb * s
    lanes = GROUP * 64

    @pl.when(i == 0)
    def _():
        copies = []
        for j in range(n):
            src = own if j == 0 else wall.at[j - 1]
            for k in range(4):
                at = pl.ds(k * width, width)
                dst = wo.at[pl.ds(j * width, width)] if k == 3 else wq.at[pl.ds(k * n * width + j * width, width)]
                copies.append(pltpu.make_async_copy(src.at[at], dst, sems.at[j, k]))
        for copy in copies:
            copy.start()
        acc[...] = jnp.zeros_like(acc)
        gacc[...] = jnp.zeros_like(gacc)
        for copy in copies:
            copy.wait()

    wide = states[...].reshape(rows, dim).astype(F32)
    inv = lax.rsqrt(jnp.mean(wide * wide, axis=-1, keepdims=True) + 1e-06)
    unit = wide * inv
    normed = (unit * gain[...]).astype(BF)
    for k in range(3):
        cols = pl.ds(k * dim, dim)
        proj[:, cols] = dot(normed, wq[cols, :], 1, 1).astype(BF)
    pos = lax.broadcasted_iota(jnp.int32, (s, dim), 0)
    mcot = jnp.concatenate(
        [jnp.where(pos < LEVELS * hist[i * nb + b], cot[b].astype(F32), 0.0) for b in range(nb)], axis=0
    ).astype(BF)
    gctx[...] = dot(mcot, wo[...], 1, 1).astype(BF)

    lane = lax.broadcasted_iota(jnp.int32, (s, lanes), 1) // 64
    key_pos = lax.broadcasted_iota(jnp.int32, (GROUP, s, s), 1)

    def spread(x):
        x = x.astype(F32)
        return jnp.concatenate([jnp.where(lane == h, x, 0.0).astype(BF) for h in range(GROUP)], axis=0)

    def fold(x):
        out = x[(GROUP - 1) * s :]
        for h in range(GROUP - 1):
            out = jnp.where(lane == h, x[h * s : (h + 1) * s], out)
        return out.astype(BF)

    @pl.loop(0, nb)
    def _(b):
        at = pl.ds(pl.multiple_of(b * s, 16), s)
        keep = key_pos < LEVELS * hist[i * nb + b]
        for g in range(dim // lanes):
            cols = [pl.ds(k * dim + g * lanes, lanes) for k in range(3)]
            here = pl.ds(g * lanes, lanes)
            q, gc = proj[at, cols[0]], gctx[at, here]
            kk, vv = spread(proj[at, cols[1]]), spread(proj[at, cols[2]])
            sc = dot(kk, q, 1, 1).reshape(GROUP, s, s)
            sc = jnp.where(keep, sc, -1e30)
            ex = jnp.exp(sc - jnp.max(sc, axis=1, keepdims=True))
            prob = ex * (1.0 / jnp.sum(ex, axis=1, keepdims=True))
            pb = prob.reshape(GROUP * s, s).astype(BF)
            ctx[at, here] = dot(pb, vv, 0, 0).astype(BF)
            gp = dot(vv, gc, 1, 1).reshape(GROUP, s, s)
            delta = jnp.sum(prob * gp, axis=1, keepdims=True)
            ds = (prob * (gp - delta)).reshape(GROUP * s, s).astype(BF)
            gproj[at, cols[0]] = dot(ds, kk, 0, 0).astype(BF)
            gproj[at, cols[1]] = fold(dot(ds, q, 1, 0))
            gproj[at, cols[2]] = fold(dot(pb, gc, 1, 0))

    att[...] = (wide + dot(ctx[...], wo[...], 1, 0)).astype(BF).reshape(nb, s, dim)
    gn = dot(gproj[...], wq[...], 1, 0)
    for k in range(3):
        acc[:, k * lanes : (k + 1) * lanes] += dot(normed, gproj[:, k * dim : k * dim + lanes], 0, 0)
    acc[:, 3 * lanes :] += dot(mcot, ctx[:, :lanes], 0, 0)
    gacc[...] += jnp.sum((gn * unit).reshape(rows // 8, 8, dim), axis=0)
    gu = gn * gain[...]
    corr = jnp.mean(gu * unit, axis=-1, keepdims=True)
    gst[...] = (mcot.astype(F32) + inv * (gu - unit * corr)).astype(BF).reshape(nb, s, dim)

    @pl.when(i == pl.num_programs(0) - 1)
    def _():
        total = jnp.sum(gacc[...], axis=0, keepdims=True)
        column = jnp.broadcast_to(total, (128, dim)).T
        high = column.astype(BF).astype(F32)
        at = lax.broadcasted_iota(jnp.int32, (dim, 128), 1)
        last = slice(4 * lanes - 128, 4 * lanes)
        acc[:, last] = jnp.where(at < 64, acc[:, last], jnp.where(at < 96, high, column - high))
        _, half, piece, _ = part.shape
        for t in range(2 * half):
            part[t % 2, t // 2] = acc[t * piece : (t + 1) * piece, :].astype(BF)


def work(states, hist, gain, own, wall, cot, n, nd):
    count, s, dim = states.shape
    nb = 4 if count % 4 == 0 else 1
    rows, lanes = nb * s, GROUP * 64
    width = dim // n
    block = pl.BlockSpec((nb, s, dim), lambda i, *_: (i, 0, 0))
    piece = (2, nd // 2, dim // nd, 4 * lanes)
    return pl.pallas_call(
        functools.partial(work_kernel, nb, n, width),
        out_shape=(
            jax.ShapeDtypeStruct(states.shape, BF),
            jax.ShapeDtypeStruct(states.shape, BF),
            jax.ShapeDtypeStruct(piece, BF),
        ),
        grid_spec=pltpu.PrefetchScalarGridSpec(
            num_scalar_prefetch=1,
            grid=(count // nb,),
            in_specs=[
                block,
                block,
                pl.BlockSpec((1, dim), lambda i, *_: (0, 0)),
                pl.BlockSpec(memory_space=pl.ANY),
                pl.BlockSpec(memory_space=pl.ANY),
            ],
            out_specs=[block, block, pl.BlockSpec(piece, lambda i, *_: (0, 0, 0, 0))],
            scratch_shapes=[
                pltpu.VMEM((3 * dim, dim), BF),
                pltpu.VMEM((dim, dim), BF),
                pltpu.VMEM((dim, 4 * lanes), F32),
                pltpu.VMEM((8, dim), F32),
                pltpu.VMEM((rows, 3 * dim), BF),
                pltpu.VMEM((rows, 3 * dim), BF),
                pltpu.VMEM((rows, dim), BF),
                pltpu.VMEM((rows, dim), BF),
                pltpu.SemaphoreType.DMA((n, 4)),
            ],
        ),
        compiler_params=pltpu.CompilerParams(
            dimension_semantics=("arbitrary",), vmem_limit_bytes=56 * 1024 * 1024
        ),
        name="work",
    )(hist, states, cot, gain.reshape(1, dim), own, wall)


def body(nd, n, states, hist_len, norm_gain, qkv_weight, output_weight, cotangent):
    dim, _, heads, size = qkv_weight.shape
    width = heads * size
    lanes = GROUP * 64
    own = jnp.concatenate([qkv_weight.reshape(dim, 3 * width).T, output_weight.reshape(width, dim)], axis=0)
    wall = gather(own.reshape(PIECES, 4 * width // PIECES, dim), n).reshape(n - 1, 4 * width, dim)
    attended, grad_states, part = work(states, hist_len, norm_gain, own, wall, cotangent, n, nd)
    summed = scatter(part)
    grads = summed.reshape(dim // nd, 4, lanes)
    grad_qkv = grads[:, :3, :width].reshape(dim // nd, 3, heads, size)
    grad_out = grads[:, 3, :width].T.reshape(heads, size, dim // nd)
    grad_gain = grads[:, 3, 192] + grads[:, 3, 224]
    return attended, grad_states, grad_qkv, grad_out, grad_gain


def solution(mesh):
    placed = (
        P("dp", None, None),
        P("dp"),
        P(),
        P(None, None, "mp", None),
        P("mp", None, None),
        P("dp", None, None),
    )
    return jax.shard_map(
        functools.partial(body, mesh.shape["dp"], mesh.shape["mp"]),
        mesh=mesh,
        in_specs=placed,
        out_specs=(
            P("dp", None, None),
            P("dp", None, None),
            P("dp", None, "mp", None),
            P("mp", None, "dp"),
            P("dp"),
        ),
        check_vma=False,
    )
```

time: 290 us -> 123 us (0.42)
  waiting for transfers between devices: 207 us -> 0 us
  Pallas kernels: 0 us -> 114 us
  matrix products: 26.7 us -> 0 us
  between operations: 16.3 us -> 0.67 us
  blocking collectives: 13.8 us -> 0 us
  local copies, waits for them, and re-layouts: 13.8 us -> 4.6 us
  other arithmetic: 12 us -> 2.92 us
    psum x2 -> x0, waiting for transfers between devices: 149 us -> none  [the longest x1 83.2 us: body(): grad_normed = lax.psum(partial_normed, 'mp')]
    pallas_call x0 -> x3, Pallas kernels: none -> 114 us  [the longest x1 60 us: work(): pl.pallas_call(functools.partial(work_kernel, nb, n, width), out_shape=(j...]
    unnamed x6 -> x0, waiting for transfers between devices: 57.7 us -> none
    dot_general x11 -> x0, matrix products: 23.1 us -> none  [the longest x1 5.38 us: body(): jnp.einsum('bschk,dchk->bsd', grad_proj, qkv_weight, preferred_element_ty...]
    unnamed x1 -> x0, blocking collectives: 13.8 us -> none
    unnamed x32 -> x2, local copies, waits for them, and re-layouts: 13.8 us -> 0.15 us
    convert_element_type x2 -> x0, other arithmetic: 5.78 us -> none  [the longest x1 5.32 us: body(): (wide_cot + inv_rms * (unit_grad - unit * row_corr)).astype(jnp.bfloat16)]
    reduce_sum x2 -> x0, other arithmetic: 5.28 us -> none  [the longest x1 3.25 us: body(): local_gain = jnp.sum(grad_normed * unit, axis=(0, 1))]
  transfers between devices with their start and end apart: 4 -> 0, of which waited for: 4 -> 0; matrix products, arithmetic and copies ran while one was open for 10% -> 0% of each run, Pallas kernels for 0% -> 0%
where the time goes in v1:
time: 123 us
  Pallas kernels  114 us (93%)
  local copies, waits for them, and re-layouts  4.6 us (4%)
  other arithmetic  2.92 us (2%)
    pallas_call x1, Pallas kernels, work(): pl.pallas_call(functools.partial(work_kernel, nb, n, width), out_shape=(j...  60 us
    pallas_call x1, Pallas kernels, gather(): pl.pallas_call(functools.partial(gather_kernel, n), out_shape=jax.ShapeDt...  38.4 us
    pallas_call x1, Pallas kernels, scatter(): pl.pallas_call(functools.partial(scatter_kernel, half), out_shape=jax.Sha...  16.1 us

profile of v1, /device:TPU:0, one launch (start us, length us, event | category | flops | bytes accessed | tf_op | source)
XLA Modules:
  0.0 122.6 jit_solution(11289969587438181005)
XLA Ops:
  0.6 1.3 %reshape.35.gain = f32[1,768]{1,0:T(1,128)} reshape(f32[768]{0:T(1024)} %param.8) | data formatting | bytes 6144 | tf_op jit(solution)/shard_map/reshape | solution.py:277
  1.9 2.4 %pad_maximum_fusion.own = bf16[768,768]{1,0:T(8,128)(2,1)} fusion(bf16[192,768]{1,0:T(8,128)(2,1)} %bitcast.20, bf16[576,768]{1,0:T(8,128)(2,1)} %bitcast.19), kind=kLoop, calls=%fused_computation | loop fusion | flops 2359296 | bytes 2359296 | tf_op jit(solution)/shard_map/concatenate | solution.py:284
  4.3 38.4 %gather.1 = bf16[3,8,96,768]{3,2,1,0:T(8,128)(2,1)} custom-call(bf16[8,96,768]{2,1,0:T(8,128)(2,1)} %bitcast.17), custom_call_target="tpu_custom_call" | custom-call | tf_op jit(solution)/shard_map/gather/pallas_call | solution.py:76
  42.7 60.0 %work.1 = (bf16[16,80,768]{2,1,0:T(8,128)(2,1)}, bf16[16,80,768]{2,1,0:T(8,128)(2,1)}, bf16[2,4,96,1024]{3,2,1,0:T(8,128)(2,1)}) custom-call(s32[16]{0:T(128)} %hist.1, bf16[16,80,768]{2,1,0:T(8,128)(2,1)} %states.1, bf16[16,80,768]{2,1,0:T(8,128)(2,1)} %cot.1, f32[1,768]{1,0:T(1,128)} %reshape.35.gain, bf16[768,768]{1,0:T(8,128)(2,1)} %pad_maximum_fusion.own, ...), custom_call_target="tpu_custom_call" | custom-call | tf_op jit(solution)/shard_map/work/pallas_call | solution.py:243
  102.6 16.1 %scatter.1 = f32[96,1024]{1,0:T(8,128)} custom-call(bf16[2,4,96,1024]{3,2,1,0:T(8,128)(2,1)} %get-tuple-element.10.part), custom_call_target="tpu_custom_call" | custom-call | tf_op jit(solution)/shard_map/scatter/pallas_call | solution.py:123
  118.7 1.2 reshape.40
  119.9 0.1 slice.17
  120.0 0.7 copy.18
  120.8 0.3 fusion
  121.0 0.1 copy.17
  121.1 0.1 copy.16
  121.2 0.5 add_bitcast_fusion
  121.7 0.9 copy.11

commit v2 on v1

--- a/solution.py
+++ b/solution.py
@@ -8,8 +8,9 @@
 from jax.sharding import PartitionSpec as P
 
 LEVELS = 4
-PIECES = 8
+PIECES = 16
 GROUP = 4
+PACK = 2
 BF = jnp.bfloat16
 F32 = jnp.float32
 MESH = pl.DeviceIdType.MESH
@@ -25,10 +26,9 @@
     )
 
 
-def gather_kernel(n, own, wall, s_z, r_z, s_xy, r_xy, s_c, r_c):
+def gather_kernel(n, own, wall, s_z, r_z, s_x, r_x, s_d, r_d, s_c, r_c):
     d, z = lax.axis_index("dp"), lax.axis_index("mp")
     c, bx, by = d % 2, (d // 2) % 2, (d // 4) % 2
-    par = (bx + by) % 2
     partner = (d + 1 - 2 * c, z)
     across = ((d + 2 - 4 * bx, z), (d + 4 - 8 * by, z))
     barrier = pltpu.get_barrier_semaphore()
@@ -37,9 +37,12 @@
         pl.semaphore_signal(barrier, inc=1, device_id=device, device_id_type=MESH)
     pl.semaphore_wait(barrier, len(greet))
 
-    mine = [4 * par + 2 * i + c for i in range(2)]
-    theirs = [4 * (1 - par) + 2 * i + c for i in range(2)]
-    far = [4 * par + 2 * i + 1 - c for i in range(2)] + [4 * (1 - par) + 2 * i + 1 - c for i in range(2)]
+    def place(x, y, core):
+        return 4 * (x + 2 * y) + 2 * core
+
+    mine = place(bx, by, c)
+    sides = (place(1 - bx, by, c), place(bx, 1 - by, c))
+    diag = place(1 - bx, 1 - by, c)
     order = [j for j in (1, n - 1) if j < n] + [j for j in range(2, n - 1)]
     sends = []
 
@@ -48,37 +51,47 @@
         copy.start()
         sends.append(copy)
 
-    for j in order:
+    def arrived(spot, rsem):
+        remote(spot, spot, rsem, rsem, partner).wait_recv()
+
+    for j in order:
+        go(own.at[pl.ds(mine, 2)], wall.at[j - 1, pl.ds(mine, 2)], s_z.at[j - 1], r_z.at[j - 1], (d, (z + n - j) % n))
+    for j in order:
+        spot = wall.at[j - 1, pl.ds(mine, 2)]
+        arrived(spot, r_z.at[j - 1])
         for i in range(2):
-            go(own.at[mine[i]], wall.at[j - 1, mine[i]], s_z.at[i, j - 1], r_z.at[i, j - 1], (d, (z + n - j) % n))
+            go(spot, spot, s_x.at[i, j - 1], r_x.at[i, j - 1], across[i])
+        go(spot, spot, s_c.at[0, j - 1], r_c.at[0, j - 1], partner)
     for j in order:
         for i in range(2):
-            spot = wall.at[j - 1, mine[i]]
-            remote(spot, spot, s_z.at[i, j - 1], r_z.at[i, j - 1], partner).wait_recv()
-            go(spot, spot, s_xy.at[i, j - 1], r_xy.at[i, j - 1], across[i])
-            go(spot, spot, s_c.at[i, j - 1], r_c.at[i, j - 1], partner)
+            spot = wall.at[j - 1, pl.ds(sides[i], 2)]
+            arrived(spot, r_x.at[i, j - 1])
+            piece = wall.at[j - 1, sides[i] + i]
+            go(piece, piece, s_d.at[i, j - 1], r_d.at[i, j - 1], across[1 - i])
+            go(spot, spot, s_c.at[1 + i, j - 1], r_c.at[1 + i, j - 1], partner)
     for j in order:
         for i in range(2):
-            spot = wall.at[j - 1, theirs[i]]
-            remote(spot, spot, s_xy.at[i, j - 1], r_xy.at[i, j - 1], partner).wait_recv()
-            go(spot, spot, s_c.at[2 + i, j - 1], r_c.at[2 + i, j - 1], partner)
-    for j in order:
-        for i in range(4):
-            spot = wall.at[j - 1, far[i]]
-            remote(spot, spot, s_c.at[i, j - 1], r_c.at[i, j - 1], partner).wait_recv()
+            piece = wall.at[j - 1, diag + i]
+            arrived(piece, r_d.at[i, j - 1])
+            go(piece, piece, s_c.at[3 + i, j - 1], r_c.at[3 + i, j - 1], partner)
+    flip = 2 - 4 * c
+    for j in order:
+        for k, spot in enumerate((mine, sides[0], sides[1])):
+            arrived(wall.at[j - 1, pl.ds(spot + flip, 2)], r_c.at[k, j - 1])
+        for i in range(2):
+            arrived(wall.at[j - 1, diag + i + flip], r_c.at[3 + i, j - 1])
     for copy in sends:
         copy.wait_send()
 
 
 def gather(own, n):
-    pairs = pltpu.SemaphoreType.DMA((2, n - 1))
-    quads = pltpu.SemaphoreType.DMA((4, n - 1))
+    one, two, five = (pltpu.SemaphoreType.DMA(k + (n - 1,)) for k in ((), (2,), (5,)))
     return pl.pallas_call(
         functools.partial(gather_kernel, n),
         out_shape=jax.ShapeDtypeStruct((n - 1,) + own.shape, own.dtype),
         in_specs=[pl.BlockSpec(memory_space=pl.ANY)],
         out_specs=pl.BlockSpec(memory_space=pl.ANY),
-        scratch_shapes=[pairs, pairs, pairs, pairs, quads, quads],
+        scratch_shapes=[one, one, two, two, two, two, five, five],
         compiler_params=pltpu.CompilerParams(collective_id=1, has_side_effects=True),
         name="gather",
     )(own)
@@ -175,37 +188,39 @@
     ).astype(BF)
     gctx[...] = dot(mcot, wo[...], 1, 1).astype(BF)
 
-    lane = lax.broadcasted_iota(jnp.int32, (s, lanes), 1) // 64
-    key_pos = lax.broadcasted_iota(jnp.int32, (GROUP, s, s), 1)
+    pack = PACK * 64
+    lane = lax.broadcasted_iota(jnp.int32, (s, pack), 1) // 64
+    key_pos = lax.broadcasted_iota(jnp.int32, (PACK, s, s), 1)
+
+    only = [(lane == h).astype(F32).astype(BF) for h in range(PACK)]
 
     def spread(x):
-        x = x.astype(F32)
-        return jnp.concatenate([jnp.where(lane == h, x, 0.0).astype(BF) for h in range(GROUP)], axis=0)
+        return jnp.concatenate([x * only[h] for h in range(PACK)], axis=0)
 
     def fold(x):
-        out = x[(GROUP - 1) * s :]
-        for h in range(GROUP - 1):
+        out = x[(PACK - 1) * s :]
+        for h in range(PACK - 1):
             out = jnp.where(lane == h, x[h * s : (h + 1) * s], out)
         return out.astype(BF)
 
-    @pl.loop(0, nb)
+    @pl.loop(0, nb, unroll=4)
     def _(b):
         at = pl.ds(pl.multiple_of(b * s, 16), s)
         keep = key_pos < LEVELS * hist[i * nb + b]
-        for g in range(dim // lanes):
-            cols = [pl.ds(k * dim + g * lanes, lanes) for k in range(3)]
-            here = pl.ds(g * lanes, lanes)
+        for g in range(dim // pack):
+            cols = [pl.ds(k * dim + g * pack, pack) for k in range(3)]
+            here = pl.ds(g * pack, pack)
             q, gc = proj[at, cols[0]], gctx[at, here]
             kk, vv = spread(proj[at, cols[1]]), spread(proj[at, cols[2]])
-            sc = dot(kk, q, 1, 1).reshape(GROUP, s, s)
+            sc = dot(kk, q, 1, 1).reshape(PACK, s, s)
             sc = jnp.where(keep, sc, -1e30)
             ex = jnp.exp(sc - jnp.max(sc, axis=1, keepdims=True))
             prob = ex * (1.0 / jnp.sum(ex, axis=1, keepdims=True))
-            pb = prob.reshape(GROUP * s, s).astype(BF)
+            pb = prob.reshape(PACK * s, s).astype(BF)
             ctx[at, here] = dot(pb, vv, 0, 0).astype(BF)
-            gp = dot(vv, gc, 1, 1).reshape(GROUP, s, s)
+            gp = dot(vv, gc, 1, 1).reshape(PACK, s, s)
             delta = jnp.sum(prob * gp, axis=1, keepdims=True)
-            ds = (prob * (gp - delta)).reshape(GROUP * s, s).astype(BF)
+            ds = (prob * (gp - delta)).reshape(PACK * s, s).astype(BF)
             gproj[at, cols[0]] = dot(ds, kk, 0, 0).astype(BF)
             gproj[at, cols[1]] = fold(dot(ds, q, 1, 0))
             gproj[at, cols[2]] = fold(dot(pb, gc, 1, 0))

time: 123 us -> 99.8 us (0.81)
  Pallas kernels: 114 us -> 91.3 us
    pallas_call x1, Pallas kernels: 60 us -> 44.3 us  [work(): pl.pallas_call(functools.partial(work_kernel, nb, n, width), out_shape=(j...]
    pallas_call x1, Pallas kernels: 38.4 us -> 31.5 us  [gather(): pl.pallas_call(functools.partial(gather_kernel, n), out_shape=jax.ShapeDt...]
where the time goes in v2:
time: 99.8 us; the launch traced here: 99.5 us
  Pallas kernels  91.3 us (91%)
  local copies, waits for them, and re-layouts  4.6 us (5%)
  other arithmetic  2.92 us (3%)
    pallas_call x1, Pallas kernels, work(): pl.pallas_call(functools.partial(work_kernel, nb, n, width), out_shape=(j...  44.3 us
    pallas_call x1, Pallas kernels, gather(): pl.pallas_call(functools.partial(gather_kernel, n), out_shape=jax.ShapeDt...  31.5 us
    pallas_call x1, Pallas kernels, scatter(): pl.pallas_call(functools.partial(scatter_kernel, half), out_shape=jax.Sha...  15.4 us
    concatenate x1, other arithmetic, body(): jnp.concatenate([qkv_weight.reshape(dim, 3 * width).T, output_weight.resh...  2.39 us

profile of v2, /device:TPU:0, one launch (start us, length us, event | category | flops | bytes accessed | tf_op | source)
XLA Modules:
  0.0 99.5 jit_solution(14173943890482599783)
XLA Ops:
  0.6 1.3 %reshape.35.gain = f32[1,768]{1,0:T(1,128)} reshape(f32[768]{0:T(1024)} %param.8) | data formatting | bytes 6144 | tf_op jit(solution)/shard_map/reshape | solution.py:292
  1.9 2.4 %pad_maximum_fusion.own = bf16[768,768]{1,0:T(8,128)(2,1)} fusion(bf16[192,768]{1,0:T(8,128)(2,1)} %bitcast.20, bf16[576,768]{1,0:T(8,128)(2,1)} %bitcast.19), kind=kLoop, calls=%fused_computation | loop fusion | flops 2359296 | bytes 2359296 | tf_op jit(solution)/shard_map/concatenate | solution.py:299
  4.3 31.5 %gather.1 = bf16[3,16,48,768]{3,2,1,0:T(8,128)(2,1)} custom-call(bf16[16,48,768]{2,1,0:T(8,128)(2,1)} %bitcast.17), custom_call_target="tpu_custom_call" | custom-call | tf_op jit(solution)/shard_map/gather/pallas_call | solution.py:89
  35.8 44.3 %work.1 = (bf16[16,80,768]{2,1,0:T(8,128)(2,1)}, bf16[16,80,768]{2,1,0:T(8,128)(2,1)}, bf16[2,4,96,1024]{3,2,1,0:T(8,128)(2,1)}) custom-call(s32[16]{0:T(128)} %hist.1, bf16[16,80,768]{2,1,0:T(8,128)(2,1)} %states.1, bf16[16,80,768]{2,1,0:T(8,128)(2,1)} %cot.1, f32[1,768]{1,0:T(1,128)} %reshape.35.gain, bf16[768,768]{1,0:T(8,128)(2,1)} %pad_maximum_fusion.own, ...), custom_call_target="tpu_custom_call" | custom-call | tf_op jit(solution)/shard_map/work/pallas_call | solution.py:258
  80.1 15.4 %scatter.1 = f32[96,1024]{1,0:T(8,128)} custom-call(bf16[2,4,96,1024]{3,2,1,0:T(8,128)(2,1)} %get-tuple-element.10.part), custom_call_target="tpu_custom_call" | custom-call | tf_op jit(solution)/shard_map/scatter/pallas_call | solution.py:136
  95.6 1.2 %reshape.40 = f32[96,4,256]{2,1,0:T(4,128)S(1)} reshape(f32[96,1024]{1,0:T(8,128)} %scatter.1) | data formatting | bytes 786432 | tf_op jit(solution)/shard_map/reshape | solution.py:303
  96.8 0.1 slice.17
  96.9 0.7 copy.18
  97.6 0.3 fusion
  97.9 0.1 copy.17
  98.0 0.1 copy.16
  98.0 0.5 add_bitcast_fusion
  98.6 0.9 copy.11
